TPU v7x, 16 devices: a 4x2x1 block of a 4x4x8 slice. The times are simulated.
16 devices in a mesh: dp: 2 (over y, z), tp: 8 (over x, core).
Axes of the slice: x: 4, y: 2, z: 1, core: 2. Of those that a mesh axis runs over, the one named last changes fastest.
The devices are a block of a 4x4x8 slice.
Arguments:
- x_seq: bfloat16 [8, 2048, 4096], P('dp', 'tp'), parts along dimension 0
- ln_gain: float32 [4096], replicated
- ln_bias: float32 [4096], replicated
- w_qkv: bfloat16 [4096, 16, 3, 256], P(None, 'tp')
- w_out: bfloat16 [4096, 4096], P('tp')
- w_up: bfloat16 [4096, 16384], P(None, 'tp')
- w_down: bfloat16 [16384, 4096], P('tp')
Outputs:
- output: bfloat16 [8, 2048, 4096], P('dp', 'tp'), parts along dimension 0
There are 2 independent parts. A program takes and returns all parts, laid end to end along the dimension named above; an argument that names none is the same for every part.
All inputs are finite; a program needn't handle non-finite values.
Results may differ from a plain program's by a relative error of at most 0.011671.
Values are sent between devices in bfloat16 or wider.
A program may use at most 768 MiB of HBM per device.

v0:
```python
import functools

import jax
import jax.numpy as jnp
from jax import lax
from jax.experimental import pallas as pl
from jax.experimental.pallas import tpu as pltpu
from jax.sharding import PartitionSpec as P

LN_EPS = 1e-5
LOG2_E = 1.4426950408889634
BOTH, PARTS = (0, 1), 4
N_IN, N_OUT, LANES, WIDE = 7, 9, 128, 512
PARTNER_GROUPS, OWN_GROUPS = (0, 2, 3, 5), (1, 3, 4, 6)
NJ = 4


def any_of(value, choices):
    return functools.reduce(jnp.logical_or, [value == c for c in choices])


def layer_kernel(x_ref, gain_ref, bias_ref, wqkv_hbm, wout_hbm, wup_hbm, wdown_hbm,
                 y_ref, own_out, left_out, right_out, n_all, ho, pbuf, pout, tin,
                 wqkv, wup, wdo, gain, bias, nbuf,
                 ag_is, ag_ir, ag_ds, ag_dr, p_s, p_r, t_s, t_r, m_s, m_r,
                 w_sem, v_sem, ln_sem, a_sem, h_sem, o_sem, d_sem, pb_sem, os_sem, f_sem, y_sem, z_sem):
    batch, rows, dim = x_ref.shape
    half = rows // 2
    ff = wup.shape[1]
    attn = wdo.shape[0] - ff
    qkv_cols = wqkv.shape[1]
    n_heads = 2
    head = attn // n_heads
    n_chips = n_all.shape[1]
    seq = n_chips * 2 * rows
    ncol = dim // NJ
    f32, bf16 = jnp.float32, jnp.bfloat16

    me = lax.axis_index("tp")
    chip, core = me // 2, me % 2
    other = 1 - core
    partner = chip * 2 + other
    right = ((chip + 1) % n_chips) * 2 + core
    left = ((chip + n_chips - 1) % n_chips) * 2 + core

    def remote(src, dst, send, recv, dev):
        return pltpu.make_async_remote_copy(
            src_ref=src, dst_ref=dst, send_sem=send, recv_sem=recv,
            device_id={"tp": dev}, device_id_type=pl.DeviceIdType.MESH)

    barrier = pltpu.get_barrier_semaphore()
    for dev in (partner, right, left):
        pl.semaphore_signal(barrier, inc=1, device_id={"tp": dev}, device_id_type=pl.DeviceIdType.MESH)

    w_copies = (
        pltpu.make_async_copy(wup_hbm, wup, w_sem.at[0]),
        pltpu.make_async_copy(wdown_hbm, wdo.at[pl.ds(0, ff)], w_sem.at[1]),
        pltpu.make_async_copy(wout_hbm, wdo.at[pl.ds(ff, attn)], w_sem.at[2]),
    )
    v_copies = (pltpu.make_async_copy(gain_ref, gain, v_sem.at[0]),
                pltpu.make_async_copy(bias_ref, bias, v_sem.at[1]))
    for cp in v_copies:
        cp.start()

    def unit(u):
        g, b = u // 2, u % 2
        near = (g * (3 - g)) // 2
        off = near * (2 * b - 1) + 2 * (g // 3)
        hf = (b + near * (g - 1)) % 2
        return (chip + off + n_chips) % n_chips, hf

    def piece(s, d, hf, k):
        return n_all.at[s, d, hf, pl.ds(pl.multiple_of(k * half, half), half)]

    def ici_copy(s, u, d, hf, dev):
        return remote(piece(s, d, hf, core), piece(s, d, hf, core), ag_is.at[s, u], ag_ir.at[s, u], dev)

    def d2d_copy(s, u, d, hf, k):
        return remote(piece(s, d, hf, k), piece(s, d, hf, k), ag_ds.at[s, u], ag_dr.at[s, u], partner)

    part = rows // PARTS

    def x_load(s, buf, q):
        at = pl.ds(q * part, part)
        return pltpu.make_async_copy(x_ref.at[s, at], buf.at[at], ln_sem.at[0, q])

    def n_store(s, buf, q):
        dst = n_all.at[s, chip, q // 2, pl.ds(pl.multiple_of(core * half + (q % 2) * part, part), part)]
        return pltpu.make_async_copy(buf.at[pl.ds(q * part, part)], dst, ln_sem.at[1, q])

    def x_start(s, buf):
        for q in range(PARTS):
            x_load(s, buf, q).start()

    def normalise(s, buf, q):
        x_load(s, buf, q).wait()
        at = pl.ds(q * part, part)
        lanes, wide = LANES, WIDE
        total = jnp.zeros((part, lanes), f32)
        for c in range(0, dim, wide):
            v = buf[at, c:c + wide].astype(f32)
            for k in range(0, wide, lanes):
                total = total + v[:, k:k + lanes]
        mean = jnp.sum(total, axis=-1, keepdims=True) * (1.0 / dim)
        total = jnp.zeros((part, lanes), f32)
        for c in range(0, dim, wide):
            cen = buf[at, c:c + wide].astype(f32) - mean
            for k in range(0, wide, lanes):
                total = total + cen[:, k:k + lanes] * cen[:, k:k + lanes]
        inv = lax.rsqrt(jnp.sum(total, axis=-1, keepdims=True) * (1.0 / dim) + LN_EPS)
        for c in range(0, dim, wide):
            cen = buf[at, c:c + wide].astype(f32) - mean
            buf[at, c:c + wide] = (cen * inv * gain[:, c:c + wide] + bias[:, c:c + wide]).astype(bf16)
        n_store(s, buf, q).start()

    def ag_first(s):
        ici_copy(s, 2, chip, 0, right).start()
        ici_copy(s, 3, chip, 1, left).start()
        d2d_copy(s, 0, chip, 0, core).start()
        d2d_copy(s, 1, chip, 1, core).start()

    def ag_second(s):
        ici_copy(s, 4, chip, 1, right).start()
        ici_copy(s, 5, chip, 0, left).start()

    def forward(s, us):
        for u in us:
            d, hf = unit(u)
            with jax.named_scope(f"ici_wait_{u}"):
                ici_copy(s, u, d, hf, right).wait_recv()
            if u == 2:
                ici_copy(s, 6, d, hf, right).start()
            if u == 3:
                ici_copy(s, 7, d, hf, left).start()
            d2d_copy(s, u, d, hf, core).start()

    def block(b, second):
        near = (b * (3 - b)) // 2
        plus = (near * (1 + (2 * second - 1) * (3 - 2 * b))) // 2
        return 2 * plus, 1 + 2 * plus + b // 3

    def cols(j):
        return pl.ds(pl.multiple_of(j * ncol, ncol), ncol)

    def to_right(s, ii, j):
        return remote(pout.at[s, ii, :, cols(j)], left_out.at[s, :, cols(j)], m_s.at[s, j], m_r.at[s, j], right)

    def to_left(s, ii, j):
        return remote(pout.at[s, ii, :, cols(j)], right_out.at[s, :, cols(j)], m_s.at[s, NJ + j], m_r.at[s, NJ + j],
                      left)

    def transit(s, j, dev):
        return remote(pout.at[s, 0, :, cols(j)], tin.at[s, :, cols(j)], t_s.at[s, j], t_r.at[s, j], dev)

    def first_load(s):
        return pltpu.make_async_copy(n_all.at[s, chip, 0], nbuf.at[0], a_sem.at[0])

    def first_start(s):
        with jax.named_scope("d2d_wait"):
            d2d_copy(s, 0, chip, 0, other).wait_recv()
        first_load(s).start()

    def gelu(h):
        return (0.5 * h * (1.0 + lax.erf(h * (2.0 ** -0.5)))).astype(bf16)

    def phase_a(s, qkv):
        def scope(hbuf):
            first, later = s == 0, s > 0

            def load(u):
                d, hf = unit(u)
                return pltpu.make_async_copy(n_all.at[s, d, hf], nbuf.at[u % 2], a_sem.at[u % 2])

            def arrived(u):
                d, hf = unit(u)
                with jax.named_scope("d2d_wait"):
                    d2d_copy(s, u, d, hf, other).wait_recv()

            def hstore(u, k):
                d, hf = unit(u)
                return pltpu.make_async_copy(
                    hbuf.at[pl.ds(k * half, half)],
                    ho.at[2 * d + k, pl.ds(pl.multiple_of(hf * half, half), half), pl.ds(0, ff)],
                    h_sem.at[k])

            def project(u):
                d, hf = unit(u)
                wide = WIDE
                for c in range(0, qkv_cols, wide):
                    r = jnp.dot(nbuf[u % 2], wqkv[:, c:c + wide], preferred_element_type=f32).astype(bf16)
                    for k in BOTH:
                        pos = pl.multiple_of(d * (2 * rows) + k * rows + hf * half, half)
                        qkv[pl.ds(pos, half), c:c + wide] = r[k * half:(k + 1) * half]

            @pl.loop(0, 2 * n_chips)
            def _(u):
                odd = u % 2 == 1
                with jax.named_scope("load_wait"):
                    load(u).wait()

                @pl.when(jnp.logical_and(later, u == 4))
                def _():
                    forward(s, (6, 7))

                @pl.when(jnp.logical_or(jnp.logical_and(later, u < 7), u % 2 == 0))
                def _():
                    arrived(u + 1)
                    load(u + 1).start()

                @pl.when(later)
                def _():
                    project(u)

                @pl.when(first)
                def _():
                    @pl.when(jnp.logical_and(odd, u < 7))
                    def _():
                        x_start((u + 1) // 2, nbuf.at[0])

                    project(u)

                    @pl.when(u == 0)
                    def _():
                        w_copies[0].wait()
                        for cp in w_copies[1:]:
                            cp.start()

                    @pl.when(u >= 1)
                    def _():
                        for k in BOTH:
                            hstore(u - 1, k).wait()
                    hbuf[...] = gelu(jnp.dot(nbuf[u % 2], wup[...], preferred_element_type=f32))
                    for k in BOTH:
                        hstore(u, k).start()

                    @pl.when(u == 1)
                    def _():
                        forward(0, (2, 3))

                    @pl.when(u == 3)
                    def _():
                        forward(0, (4, 5))

                    @pl.when(u == 5)
                    def _():
                        forward(0, (6, 7))

                    @pl.when(jnp.logical_and(odd, u < 7))
                    def _():
                        with jax.named_scope("norm"):
                            for q in range(PARTS):
                                normalise((u + 1) // 2, nbuf.at[0], q)
                            for q in range(PARTS):
                                n_store((u + 1) // 2, nbuf.at[0], q).wait()

                        @pl.when(u == 1)
                        def _():
                            ag_first(1)
                            ag_second(1)
                        arrived(u + 1)
                        load(u + 1).start()

            @pl.when(first)
            def _():
                for k in BOTH:
                    hstore(7, k).wait()
        pl.run_scoped(scope, pltpu.VMEM((rows, ff), bf16))

    def phase_b(qkv):
        def ostore(t):
            return pltpu.make_async_copy(qkv.at[pl.ds(t * rows, rows), pl.ds(0, attn)],
                                         ho.at[t, :, pl.ds(ff, attn)], o_sem.at[t])
        scale = head ** -0.5

        probs = nbuf.at[1]

        def scope(*scores):
            keep = (lax.broadcasted_iota(jnp.int32, (rows, rows), 0)
                    >= lax.broadcasted_iota(jnp.int32, (rows, rows), 1))
            tasks = [(t, h) for t in range(seq // rows) for h in range(n_heads)]
            tops = {}

            def score(i):
                t, h = tasks[i]
                r0, n = t * rows, (t + 1) * rows
                q = qkv[r0:n, h * head:(h + 1) * head]
                k = qkv[0:n, attn + h * head:attn + (h + 1) * head]
                sc = lax.dot_general(q, k, (((1,), (1,)), ((), ())), preferred_element_type=f32)
                diag = jnp.where(keep, sc[:, r0:], -jnp.inf)
                top = jnp.max(diag, axis=1, keepdims=True)
                if t:
                    scores[i % 2][0, :, 0:r0] = sc[:, :r0]
                    top = jnp.maximum(top, jnp.max(sc[:, :r0], axis=1, keepdims=True))
                scores[i % 2][0, :, r0:n] = diag
                tops[i] = top

            def soften(i):
                t, h = tasks[i]
                n = (t + 1) * rows
                total = jnp.zeros((rows, rows // 2), f32)
                for c in range(0, n, rows):
                    e = jnp.exp2((scores[i % 2][0, :, c:c + rows] - tops[i]) * (scale * LOG2_E))
                    scores[i % 2][0, :, c:c + rows] = e
                    total = total + e[:, :rows // 2] + e[:, rows // 2:]
                inverse = 1.0 / jnp.sum(total, axis=1, keepdims=True)
                for c in range(0, n, rows):
                    probs[:, (i % 2) * seq + c:(i % 2) * seq + c + rows] = (
                        scores[i % 2][0, :, c:c + rows] * inverse).astype(bf16)

            def mix(i):
                t, h = tasks[i]
                r0, n = t * rows, (t + 1) * rows
                v = qkv[0:n, 2 * attn + h * head:2 * attn + (h + 1) * head]
                o = jnp.dot(probs[:, (i % 2) * seq:(i % 2) * seq + n], v, preferred_element_type=f32)
                qkv[r0:n, h * head:(h + 1) * head] = o.astype(bf16)

            score(0)
            for i in range(len(tasks)):
                if i + 1 < len(tasks):
                    score(i + 1)
                soften(i)
                mix(i)
                if i % n_heads == n_heads - 1 and tasks[i][0] % PARTS == PARTS - 1:
                    for done in range(tasks[i][0] - PARTS + 1, tasks[i][0] + 1):
                        ostore(done).start()
            for t in range(seq // rows):
                ostore(t).wait()
        pl.run_scoped(scope, pltpu.VMEM((1, rows, seq), f32), pltpu.VMEM((1, rows, seq), f32))

    def chip_of(w):
        near = (w * (3 - w)) // 2
        off = near * (3 - 2 * w) + 2 * ((3 - w) // 3)
        plus = near * (2 - w)
        return (chip + off + n_chips) % n_chips, 2 * plus, 1 + 2 * plus + w // 3

    def place_of(v):
        return (v % 3) * (2 - v % 3)

    def rows_load(s, v):
        d, _, _ = chip_of(v // 2)
        return pltpu.make_async_copy(n_all.at[s, d, v % 2], nbuf.at[place_of(v)], a_sem.at[place_of(v)])

    def rows_start(s, v):
        rows_load(s, v).start()

    def phase_d(s):
        def scope(lhs, pst, ost, tb):
            first, later, last = s == 0, s > 0, s == batch - 1

            def left_load(w, own, whole):
                d, slot_p, slot_o = chip_of(w)
                src = ho.at[2 * d + (core if own else other)]
                dst = lhs.at[slot_o if own else slot_p]
                if not whole:
                    src, dst = src.at[:, pl.ds(ff, attn)], dst.at[:, pl.ds(ff, attn)]
                return pltpu.make_async_copy(src, dst, d_sem.at[w, own])

            def left_act(w, own, act):
                @pl.when(first)
                def _():
                    act(left_load(w, own, True))

                @pl.when(later)
                def _():
                    act(left_load(w, own, False))

            def left_start(w, own):
                left_act(w, own, lambda cp: cp.start())

            def left_wait(w, own):
                left_act(w, own, lambda cp: cp.wait())

            def hide(v):
                _, slot_p, slot_o = chip_of(v // 2)
                at = pl.multiple_of((v % 2) * half, half)
                wide = WIDE
                for c in range(0, ff, wide):
                    r = gelu(jnp.dot(nbuf[place_of(v)], wup[:, c:c + wide], preferred_element_type=f32))
                    for k in BOTH:
                        own = 1 - (k + core) % 2
                        slot = slot_p + own * (slot_o - slot_p)
                        lhs[slot, pl.ds(at, half), c:c + wide] = r[k * half:(k + 1) * half]

            def nth(i, k):
                return 2 * i + k

            def swap(b, t, c):
                n = nth(t, c)
                return remote(pst.at[n], pbuf.at[s, b, n], p_s.at[n], p_r.at[s, b * NJ + n], partner)

            def pb_at(t, c):
                return nbuf.at[1, :, cols(nth(t, c))]

            def pb_load(b, t, c):
                return pltpu.make_async_copy(pbuf.at[s, b, nth(t, c)], pb_at(t, c), pb_sem.at[nth(t, c)])

            def pb_start(b, t):
                for c in BOTH:
                    with jax.named_scope("swap_wait"):
                        swap(b, t, c).wait_recv()
                    pb_load(b, t, c).start()

            def t_load(t, c):
                return pltpu.make_async_copy(tin.at[s, :, cols(nth(c, t))], tb.at[c], f_sem.at[c])

            def stored(t):
                for c in BOTH:
                    pltpu.make_async_copy(ost.at[nth(t, c)], pout.at[s, 0, :, cols(nth(c, t))],
                                          os_sem.at[nth(t, c)]).wait()

            def post(b, t):
                stored(t)

                @pl.when(b == 0)
                def _():
                    transit(s, t, right).start()
                    transit(s, 2 + t, left).start()

                @pl.when(b == 1)
                def _():
                    to_left(s, 1, t).start()
                    to_right(s, 1, 2 + t).start()

                @pl.when(b == 2)
                def _():
                    to_right(s, 2, t).start()
                    to_left(s, 2, 2 + t).start()

            def partner_step(b, t):
                @pl.when(b >= 1)
                def _():
                    for c in BOTH:
                        swap(b - 1, t, c).wait_send()

                @pl.when(jnp.logical_and(b == 2, t == 0))
                def _():
                    pb_start(1, 0)
                for c in BOTH:
                    slot_p, _ = block(b, c)
                    r = jnp.dot(lhs[slot_p], wdo[:, cols(nth(c, t))], preferred_element_type=f32)
                    pst[nth(t, c)] = r.astype(bf16)
                for c in BOTH:
                    swap(b, t, c).start()

                @pl.when(jnp.logical_and(jnp.logical_not(last), jnp.logical_and(b == 2, t == 1)))
                def _():
                    post(1, 0)

            def own_step(b, t):
                @pl.when(jnp.logical_and(b == 3, t == 0))
                def _():
                    pb_start(3, 0)

                late = jnp.logical_and(t == 0, jnp.logical_or(b == 3, jnp.logical_and(first, b == 0)))

                @pl.when(jnp.logical_and(t == 0, jnp.logical_not(late)))
                def _():
                    pb_start(b, 1)

                @pl.when(jnp.logical_and(b == 1, t == 1))
                def _():
                    pb_start(2, 0)

                @pl.when(b == 2)
                def _():
                    with jax.named_scope("transit_wait"):
                        for c in BOTH:
                            transit(s, nth(c, t), right).wait_recv()
                    for c in BOTH:
                        t_load(t, c).start()
                for c in BOTH:
                    pb_load(b, t, c).wait()
                for c in BOTH:
                    _, slot_o = block(b, c)
                    r = jnp.dot(lhs[slot_o], wdo[:, cols(nth(c, t))], preferred_element_type=f32)
                    ost[nth(t, c)] = (r + pb_at(t, c)[...].astype(f32)).astype(bf16)

                @pl.when(b == 2)
                def _():
                    for c in BOTH:
                        t_load(t, c).wait()

                        @pl.loop(0, PARTS)
                        def _(r):
                            at = pl.ds(pl.multiple_of(r * part, part), part)
                            ost[nth(t, c), at, :] = (ost[nth(t, c), at, :].astype(f32)
                                                     + tb[c, at, :].astype(f32)).astype(bf16)

                for c in BOTH:
                    @pl.when(b < 3)
                    def _():
                        pltpu.make_async_copy(ost.at[nth(t, c)], pout.at[s, b, :, cols(nth(c, t))],
                                              os_sem.at[nth(t, c)]).start()

                    @pl.when(b == 3)
                    def _():
                        pltpu.make_async_copy(ost.at[nth(t, c)], own_out.at[s, :, cols(nth(c, t))],
                                              os_sem.at[nth(t, c)]).start()

                @pl.when(late)
                def _():
                    pb_start(b, 1)

                @pl.when(jnp.logical_and(last, jnp.logical_and(b == 1, t == 0)))
                def _():
                    post(1, 0)

                @pl.when(jnp.logical_and(b == 2, t == 0))
                def _():
                    post(1, 1)

                @pl.when(jnp.logical_and(t == 1, b % 2 == 0))
                def _():
                    post(b, 0)

            for w in BOTH:
                for own in BOTH:
                    left_start(w, own)

            @pl.when(first)
            def _():
                w_copies[1].wait()
                w_copies[2].wait()

            n_groups = 7

            def since(g, k):
                return (g + 8 - k) // 8

            def step_of(g, groups):
                return sum(since(g, k) for k in groups[1:])

            def units(g):
                return 2 * since(g, 1) + since(g, 2) + 3 * since(g, 3) + 2 * since(g, 6)

            @pl.loop(0, n_groups)
            def _(g):
                @pl.when(g == 1)
                def _():
                    pb_start(0, 0)
                    left_start(2, 0)

                @pl.when(g == 2)
                def _():
                    left_start(2, 1)

                @pl.when(g == 3)
                def _():
                    left_wait(1, 1)
                    left_wait(2, 1)

                @pl.when(g == 4)
                def _():
                    left_start(3, 0)
                    left_start(3, 1)

                @pl.when(later)
                def _():
                    @pl.loop(units(g), units(g + 1))
                    def _(v):
                        with jax.named_scope("n_wait"):
                            rows_load(s, v).wait()

                        @pl.when(jnp.logical_and(v % 3 != 2, v < 2 * n_chips - 1))
                        def _():
                            rows_start(s, v + 1)

                        @pl.when(jnp.logical_and(v == 2 * n_chips - 1, s < batch - 1))
                        def _():
                            first_start(s + 1)
                        with jax.named_scope("hide"):
                            hide(v)

                        @pl.when(v % 3 == 2)
                        def _():
                            rows_start(s, v + 1)

                        @pl.when(v == 3)
                        def _():
                            post(0, 1)

                        @pl.when(v == 6)
                        def _():
                            post(2, 1)

                @pl.when(g == 0)
                def _():
                    left_wait(0, 0)

                @pl.when(g == 1)
                def _():
                    left_wait(0, 1)

                @pl.when(g == 2)
                def _():
                    left_wait(1, 0)
                    left_wait(2, 0)

                @pl.when(g == 5)
                def _():
                    left_wait(3, 0)
                    left_wait(3, 1)

                @pl.when(first)
                def _():
                    @pl.when(g == 2)
                    def _():
                        post(0, 1)

                    @pl.when(g == 5)
                    def _():
                        post(2, 1)

                    @pl.when(g == 6)
                    def _():
                        first_start(s + 1)

                @pl.loop(0, 2)
                def _(t):
                    @pl.when(any_of(g, PARTNER_GROUPS))
                    def _():
                        with jax.named_scope("partner"):
                            partner_step(step_of(g, PARTNER_GROUPS), t)

                    @pl.when(any_of(g, OWN_GROUPS))
                    def _():
                        with jax.named_scope("own"):
                            own_step(step_of(g, OWN_GROUPS), t)

                @pl.when(jnp.logical_and(s < batch - 1, g == 2))
                def _():
                    @pl.when(later)
                    def _():
                        ag_second(s + 1)
                    forward(s + 1, (2, 3))

                @pl.when(jnp.logical_and(s < batch - 1, g == n_groups - 1))
                def _():
                    forward(s + 1, (4, 5))

            stored(0)
            stored(1)
            for t in BOTH:
                for c in BOTH:
                    swap(3, t, c).wait_send()

            @pl.when(s < batch - 2)
            def _():
                ag_first(s + 2)
        pl.run_scoped(scope, pltpu.VMEM((4, rows, ff + attn), bf16), pltpu.VMEM((NJ, rows, ncol), bf16),
                      pltpu.VMEM((NJ, rows, ncol), bf16), pltpu.VMEM((2, rows, ncol), bf16))

    def opening(raw, wide):
        kinds = qkv_cols // attn
        per = qkv_cols // LANES
        slots, part_rows = raw.shape[0], raw.shape[1]
        n_parts = dim * per // part_rows
        chunk = wide.shape[0] // per
        chunks = part_rows // (chunk * per)
        xbuf = nbuf.at[1]

        def load(q):
            at = pl.ds(pl.multiple_of(q * part_rows, part_rows), part_rows)
            return pltpu.make_async_copy(wqkv_hbm.at[at], raw.at[q % slots], o_sem.at[q])

        x_start(0, xbuf)
        for q in range(slots):
            load(q).start()
        for cp in v_copies:
            cp.wait()
        with jax.named_scope("send0"):
            for q in range(PARTS):
                normalise(0, xbuf, q)
                if q == 1:
                    n_store(0, xbuf, 0).wait()
                    n_store(0, xbuf, 1).wait()
                    pl.semaphore_wait(barrier, 3)
                    ici_copy(0, 2, chip, 0, right).start()
                    d2d_copy(0, 0, chip, 0, core).start()
            n_store(0, xbuf, 2).wait()
            n_store(0, xbuf, 3).wait()
            ici_copy(0, 3, chip, 1, left).start()
            d2d_copy(0, 1, chip, 1, core).start()
            ag_second(0)
        with jax.named_scope("place"):
            @pl.loop(0, n_parts)
            def _(q):
                load(q).wait()

                @pl.loop(0, chunks)
                def _(i):
                    at = pl.ds(pl.multiple_of(i * (chunk * per), chunk * per), chunk * per)
                    wide[...] = raw[q % slots, at, :].astype(f32)
                    to = pl.ds(pl.multiple_of((q * chunks + i) * chunk, chunk), chunk)
                    for j in range(kinds):
                        for c in range(head // LANES):
                            for g in range(n_heads):
                                row = (j * (head // LANES) + c) * n_heads + g
                                col = j * attn + g * head + c * LANES
                                wqkv[to, col:col + LANES] = wide[pl.ds(row, chunk, stride=per), :].astype(bf16)

                @pl.when(q + slots < n_parts)
                def _():
                    load(q + slots).start()

                @pl.when(q == n_parts - slots)
                def _():
                    w_copies[0].start()
                    first_start(0)

    pl.run_scoped(opening, pltpu.VMEM((6, dim * (qkv_cols // LANES) // 8, LANES), bf16),
                  pltpu.VMEM((LANES * (qkv_cols // LANES), LANES), f32))

    @pl.loop(0, batch)
    def _(s):
        def scope(qkv):
            with jax.named_scope("A"):
                phase_a(s, qkv)

            @pl.when(s > 0)
            def _():
                rows_start(s, 0)
            with jax.named_scope("B"):
                phase_b(qkv)
        pl.run_scoped(scope, pltpu.VMEM((seq, qkv_cols), bf16))
        with jax.named_scope("D"):
            phase_d(s)

    def finish(buf, out):
        n_steps, depth, n_out = batch * PARTS, buf.shape[0], out.shape[0]

        def rows_at(n):
            return n // PARTS, pl.ds(pl.multiple_of((n % PARTS) * part, part), part)

        def loads(n):
            s, at = rows_at(n)
            return [pltpu.make_async_copy(src.at[s, at], buf.at[n % depth, i], y_sem.at[n % depth, i])
                    for i, src in enumerate((own_out, left_out, right_out, x_ref))]

        def store(n):
            s, at = rows_at(n)
            return pltpu.make_async_copy(out.at[n % n_out], y_ref.at[s, at], z_sem.at[n % n_out])

        def begin(n):
            @pl.when(n % PARTS == 0)
            def _():
                with jax.named_scope("last_wait"):
                    for j in range(NJ):
                        to_right(n // PARTS, 2, j).wait_recv()
                        to_left(n // PARTS, 2, j).wait_recv()
            for cp in loads(n):
                cp.start()

        def sweep(start, stop):
            for n in range(start, start + depth):
                begin(n)

            @pl.loop(start, stop)
            def _(n):
                k = n % depth
                for cp in loads(n):
                    cp.wait()

                @pl.when(n >= n_out)
                def _():
                    store(n - n_out).wait()
                for c in range(0, dim, ncol):
                    own, from_left, from_right, x = (buf[k, i, :, c:c + ncol].astype(f32) for i in range(PARTS))
                    branch = (own + from_left + from_right).astype(bf16)
                    out[n % n_out, :, c:c + ncol] = (x + branch.astype(f32)).astype(bf16)
                store(n).start()

                @pl.when(n + depth < stop)
                def _():
                    begin(n + depth)

        sweep(0, n_steps - PARTS)
        sweep(n_steps - PARTS, n_steps)
        for n in range(n_steps - n_out, n_steps):
            store(n).wait()

    with jax.named_scope("finish"):
        pl.run_scoped(finish, pltpu.VMEM((PARTS, PARTS, part, dim), bf16), pltpu.VMEM((3, part, dim), bf16))

    @pl.loop(0, batch)
    def _(s):
        for j in range(NJ):
            to_right(s, 2, j).wait_send()
            to_left(s, 2, j).wait_send()
            transit(s, j, right).wait_send()
        for u in range(2 * n_chips):
            d, hf = unit(u)
            d2d_copy(s, u, d, hf, core).wait_send()
            if u >= 2:
                ici_copy(s, u, d, hf, right).wait_send()


def layer_call(x_blk, ln_gain, ln_bias, wqkv, w_out, w_up, w_down, n_tp):
    batch, rows, dim = x_blk.shape
    ff, attn, qkv_cols = w_up.shape[1], w_out.shape[0], wqkv.shape[0] * LANES // dim
    n_chips = n_tp // 2
    ncol = dim // NJ
    bf16 = jnp.bfloat16
    dma = pltpu.SemaphoreType.DMA
    flops = 2 * batch * n_tp * rows * dim * (qkv_cols + 2 * ff + attn)
    outs = pl.pallas_call(
        layer_kernel,
        name="parallel_layer",
        out_shape=[
            jax.ShapeDtypeStruct((batch, rows, dim), bf16),
            jax.ShapeDtypeStruct((batch, rows, dim), bf16),
            jax.ShapeDtypeStruct((batch, rows, dim), bf16),
            jax.ShapeDtypeStruct((batch, rows, dim), bf16),
            jax.ShapeDtypeStruct((batch, n_chips, 2, rows, dim), bf16),
            jax.ShapeDtypeStruct((n_tp, rows, ff + attn), bf16),
            jax.ShapeDtypeStruct((batch, 4, NJ, rows, ncol), bf16),
            jax.ShapeDtypeStruct((batch, 3, rows, dim), bf16),
            jax.ShapeDtypeStruct((batch, rows, dim), bf16),
        ],
        in_specs=[pl.BlockSpec(memory_space=pl.ANY)] * N_IN,
        out_specs=[pl.BlockSpec(memory_space=pl.ANY)] * N_OUT,
        scratch_shapes=[
            pltpu.VMEM((dim, qkv_cols), bf16), pltpu.VMEM((dim, ff), bf16), pltpu.VMEM((ff + attn, dim), bf16),
            pltpu.VMEM((1, dim), jnp.float32), pltpu.VMEM((1, dim), jnp.float32), pltpu.VMEM((2, rows, dim), bf16),
            dma((batch, 8)), dma((batch, 8)), dma((batch, 8)), dma((batch, 8)),
            dma((NJ,)), dma((batch, 4 * NJ)), dma((batch, NJ)), dma((batch, NJ)),
            dma((batch, 2 * NJ)), dma((batch, 2 * NJ)),
            dma((3,)), dma((2,)), dma((2, 4)), dma((2,)), dma((2,)), dma((n_tp,)), dma((4, 2)), dma((NJ,)), dma((NJ,)),
            dma((2,)), dma((PARTS, PARTS)), dma((3,)),
        ],
        compiler_params=pltpu.CompilerParams(
            collective_id=0, has_side_effects=True, vmem_limit_bytes=67043328),
        cost_estimate=pl.CostEstimate(flops=flops, bytes_accessed=256 << 20, transcendentals=0),
    )(x_blk, ln_gain.reshape(1, dim), ln_bias.reshape(1, dim), wqkv, w_out, w_up, w_down)
    return outs[0]


def solution(mesh):
    n_tp = mesh.shape["tp"]

    def local_layer(x_blk, ln_gain, ln_bias, w_qkv, w_out, w_up, w_down):
        dim = x_blk.shape[2]
        groups, kinds, head = w_qkv.shape[1:]
        wqkv = w_qkv.reshape(dim, groups, kinds, head // LANES, LANES).transpose(0, 2, 3, 1, 4).reshape(-1, LANES)
        return layer_call(x_blk, ln_gain, ln_bias, wqkv, w_out, w_up, w_down, n_tp)

    return jax.shard_map(
        local_layer, mesh=mesh,
        in_specs=(P("dp", "tp", None), P(), P(), P(None, "tp", None, None),
                  P("tp", None), P(None, "tp"), P("tp", None)),
        out_specs=P("dp", "tp", None), check_vma=False)
```

profile of v0, /device:TPU:112, one launch (start us, length us, event | category | flops | bytes accessed | tf_op | source)
XLA Modules:
  0.0 583.2 jit_solution(14851585546156855184)
XLA Ops:
  0.0 575.3 %parallel_layer.1 = (bf16[4,256,4096]{2,1,0:T(8,128)(2,1)}, bf16[4,256,4096]{2,1,0:T(8,128)(2,1)}, bf16[4,256,4096]{2,1,0:T(8,128)(2,1)}, bf16[4,256,4096]{2,1,0...) custom-call(bf16[4,256,4096]{2,1,0:T(8,128)(2,1)} %x_ref.1, ...), custom_call_target="tpu_custom_call" | custom-call | flops 412316860416 | bytes 268435456 | tf_op jit(solution)/shard_map/parallel_layer/pallas_call | solution.py:806
  575.3 7.9 %copy.10 = bf16[4,256,4096]{2,1,0:T(8,128)(2,1)} copy(bf16[4,256,4096]{2,1,0:T(8,128)(2,1)} %get-tuple-element.6) | data formatting | bytes 16777216
where the time goes:
time: 584 us; the launch traced here: 583 us
  Pallas kernels  575 us (98%)
  local copies, waits for them, and re-layouts  7.89 us (1%)
    pallas_call x1, Pallas kernels, layer_call(): pl.pallas_call(layer_kernel, name='parallel_layer', out_shape=[jax.ShapeD...  575 us

commit v1 on v0

--- a/solution.py
+++ b/solution.py
@@ -513,6 +513,10 @@
                 def _():
                     post(b, 0)
 
+            @pl.when(s == batch - 2)
+            def _():
+                ag_second(s + 1)
+
             for w in BOTH:
                 for own in BOTH:
                     left_start(w, own)
@@ -629,7 +633,7 @@
 
                 @pl.when(jnp.logical_and(s < batch - 1, g == 2))
                 def _():
-                    @pl.when(later)
+                    @pl.when(jnp.logical_and(later, s < batch - 2))
                     def _():
                         ag_second(s + 1)
                     forward(s + 1, (2, 3))

time: 584 us -> 604 us (1.034)
  Pallas kernels: 575 us -> 595 us
    pallas_call x1, Pallas kernels: 575 us -> 595 us  [layer_call(): pl.pallas_call(layer_kernel, name='parallel_layer', out_shape=[jax.ShapeD...]
where the time goes in v1:
time: 604 us; the launch traced here: 603 us
  Pallas kernels  595 us (99%)
  local copies, waits for them, and re-layouts  7.89 us (1%)
    pallas_call x1, Pallas kernels, layer_call(): pl.pallas_call(layer_kernel, name='parallel_layer', out_shape=[jax.ShapeD...  595 us

profile of v1, /device:TPU:112, one launch (start us, length us, event | category | flops | bytes accessed | tf_op | source)
XLA Modules:
  0.0 603.3 jit_solution(14268737704216847382)
XLA Ops:
  0.0 595.4 %parallel_layer.1 = (bf16[4,256,4096]{2,1,0:T(8,128)(2,1)}, bf16[4,256,4096]{2,1,0:T(8,128)(2,1)}, bf16[4,256,4096]{2,1,0:T(8,128)(2,1)}, bf16[4,256,4096]{2,1,0...) custom-call(bf16[4,256,4096]{2,1,0:T(8,128)(2,1)} %x_ref.1, ...), custom_call_target="tpu_custom_call" | custom-call | flops 412316860416 | bytes 268435456 | tf_op jit(solution)/shard_map/parallel_layer/pallas_call | solution.py:810
  595.4 7.9 %copy.10 = bf16[4,256,4096]{2,1,0:T(8,128)(2,1)} copy(bf16[4,256,4096]{2,1,0:T(8,128)(2,1)} %get-tuple-element.6) | data formatting | bytes 16777216
